TPU v7x, 32 devices: a whole 2x2x4 slice. The times are simulated.
32 devices in a mesh: ga: 8 (over z, y), band: 4 (over x, core).
Axes of the slice: x: 2, y: 2, z: 4, core: 2. Of those that a mesh axis runs over, the one named last changes fastest.
Arguments:
- coeffs: bfloat16 [2048, 128], P('ga', 'band'), may hold values from -6 to 6
- coupling: bfloat16 [12288, 12288], P('ga', 'band'), may hold values from -0.21875 to 0.21875
- miller: int32 [3, 2048], P(None, 'ga'), may hold values from -24 to 24
- species: int32 [1024], replicated, may hold values from 0 to 3
- proj_atom: int32 [12288], replicated, may hold values from 0 to 1023, as said below
- positions: float32 [3, 1024], replicated, may hold values from 0 to 1
- radial: float32 [12, 128], replicated, may hold values from -8 to 8
Outputs:
- result: bfloat16 [2048, 128], P('ga', 'band')
Inputs may be any that keep to these rules, and one draw needn't show every extreme that they name: `proj_atom`: projector p has channel p mod 12; each atom owns 12 consecutive projectors.
All inputs are finite; a program needn't handle non-finite values.
Results may differ from a plain program's by a relative error of at most 0.008.
Values may be sent and summed in bfloat16 or wider, within the bound.
No kernel may reach another device: no remote copies, remote signals or barrier semaphores. Data moves between devices by JAX's collectives and lax.ppermute only.
A program may use at most 128 MiB of HBM per device.

v0:
```python
import math
import jax
import jax.numpy as jnp
from jax import lax
from jax.sharding import PartitionSpec as P

NCH = 12
SHELLS = 3
KINDS = 4
QBINS = 128
MMAX = 24
NPROJ = 12288


def radial_values(miller_block, radial):
    mf = miller_block.astype(jnp.float32)
    qval = (mf[0] * mf[0] + mf[1] * mf[1] + mf[2] * mf[2]) * ((QBINS - 1) / (3.0 * MMAX * MMAX))
    knots = jnp.arange(QBINS, dtype=jnp.int32).astype(jnp.float32)
    hats = jnp.maximum(0.0, 1.0 - jnp.abs(qval[:, None] - knots[None, :]))
    return jnp.dot(hats, radial.T, precision=lax.Precision.HIGHEST)


def beta_columns(miller_block, radval, species, proj_atom, positions, start, count, scale):
    mf = miller_block.astype(jnp.float32)
    atoms = lax.dynamic_slice_in_dim(proj_atom, jnp.asarray(start).astype(jnp.int32), count)
    channel = (jnp.asarray(start).astype(jnp.int32) + jnp.arange(count, dtype=jnp.int32)) % NCH
    shell = channel // 4
    comp = channel % 4
    kind = jnp.take(species, atoms)
    column = kind * SHELLS + shell
    select = (column[None, :] == jnp.arange(KINDS * SHELLS, dtype=jnp.int32)[:, None]).astype(
        jnp.float32
    )
    radpart = jnp.dot(radval, select, precision=lax.Precision.HIGHEST)
    place = jnp.take(positions, atoms, axis=1)
    theta = (
        2.0
        * math.pi
        * (
            mf[0][:, None] * place[0][None, :]
            + mf[1][:, None] * place[1][None, :]
            + mf[2][:, None] * place[2][None, :]
        )
    )
    unit = mf / MMAX
    angular = jnp.where(
        comp[None, :] == 1,
        unit[0][:, None],
        jnp.where(
            comp[None, :] == 2,
            unit[1][:, None],
            jnp.where(comp[None, :] == 3, unit[2][:, None], jnp.ones_like(theta)),
        ),
    )
    phase = jnp.where(comp[None, :] == 0, jnp.cos(theta), jnp.sin(theta))
    return (radpart * angular * phase * scale).astype(jnp.bfloat16)


def beta_atoms(miller_block, radval, species, proj_atom, positions, start, count, scale):
    mf = miller_block.astype(jnp.float32)
    npw = mf.shape[1]
    natoms = count // NCH
    owners = lax.dynamic_slice_in_dim(proj_atom, jnp.asarray(start).astype(jnp.int32), count)
    atoms = owners.reshape(natoms, NCH)[:, 0]
    kind = jnp.take(species, atoms)
    column = kind[:, None] * SHELLS + jnp.arange(SHELLS, dtype=jnp.int32)[None, :]
    select = (
        column.reshape(-1)[None, :] == jnp.arange(KINDS * SHELLS, dtype=jnp.int32)[:, None]
    ).astype(jnp.float32)
    radpart = jnp.dot(radval, select, precision=lax.Precision.HIGHEST).reshape(npw, natoms, SHELLS)
    place = jnp.take(positions, atoms, axis=1)
    theta = (
        2.0
        * math.pi
        * (
            mf[0][:, None] * place[0][None, :]
            + mf[1][:, None] * place[1][None, :]
            + mf[2][:, None] * place[2][None, :]
        )
    )
    cosine = jnp.cos(theta)
    sine = jnp.sin(theta)
    unit = mf / MMAX
    ones = jnp.ones((npw, natoms), jnp.float32)
    angular = jnp.stack(
        [
            ones,
            jnp.broadcast_to(unit[0][:, None], (npw, natoms)),
            jnp.broadcast_to(unit[1][:, None], (npw, natoms)),
            jnp.broadcast_to(unit[2][:, None], (npw, natoms)),
        ],
        axis=2,
    )
    phase = jnp.stack([cosine, sine, sine, sine], axis=2)
    values = radpart[:, :, :, None] * angular[:, :, None, :] * phase[:, :, None, :] * scale
    return values.reshape(npw, count).astype(jnp.bfloat16)


def make_beta(miller_block, radval, species, proj_atom, positions, start, count, scale, aligned):
    if aligned and count % NCH == 0:
        return beta_atoms(miller_block, radval, species, proj_atom, positions, start, count, scale)
    return beta_columns(miller_block, radval, species, proj_atom, positions, start, count, scale)


def block_size(count):
    width = 1
    for cand in range(min(count, 768), 0, -1):
        if count % cand == 0:
            width = cand
            break
    return width


def shards(coeffs, coupling, miller, species, proj_atom, positions, radial):
    scale = 1.0 / math.sqrt(coeffs.shape[0] * lax.axis_size("ga"))
    radval = radial_values(miller, radial)
    nbands = coeffs.shape[1]
    aligned = coupling.shape[0] % NCH == 0
    width = block_size(NPROJ)
    starts = width * jnp.arange(NPROJ // width, dtype=jnp.int32)

    def one_block(first):
        beta = make_beta(
            miller, radval, species, proj_atom, positions, first, width, scale, aligned
        )
        return lax.dot_general(
            beta, coeffs, (((0,), (0,)), ((), ())), preferred_element_type=jnp.float32
        )

    summed = lax.psum(lax.map(one_block, starts).reshape(NPROJ, nbands), "ga")
    proj_b = summed.astype(jnp.bfloat16)
    full_rows = lax.all_gather(coupling, "band", axis=1, tiled=True)
    mixed = jnp.dot(full_rows, proj_b, preferred_element_type=jnp.float32).astype(jnp.bfloat16)
    piece = jax.tree.map(lambda part: lax.all_gather(part, "ga", axis=0, tiled=True), mixed)
    start = jnp.int32(0)
    count = piece.shape[0]
    add_width = block_size(count)

    def step(index, acc):
        first = start + index * add_width
        beta = make_beta(
            miller, radval, species, proj_atom, positions, first, add_width, scale, aligned
        )
        rows = lax.dynamic_slice_in_dim(piece, index * add_width, add_width, 0)
        return acc + jnp.dot(beta, rows, preferred_element_type=jnp.float32)

    summed_back = lax.fori_loop(0, count // add_width, step, coeffs.astype(jnp.float32))
    return summed_back.astype(jnp.bfloat16)


def solution(mesh):
    placed = (P("ga", "band"), P("ga", "band"), P(None, "ga"), P(), P(), P(), P())
    return jax.shard_map(
        shards, mesh=mesh, in_specs=placed, out_specs=P("ga", "band"), check_vma=False
    )
```

profile of v0, /device:TPU:0, one launch (start us, length us, event | category | flops | bytes accessed | tf_op | source)
XLA Modules:
  0.0 415.7 jit_solution(7675885683890201779)
XLA Ops:
  7.9 172.2 %while.27 = (s32[]{:T(128)}, f32[16,768,32]{1,0,2:T(8,128)S(1)}, s32[16]{0:T(128)S(1)}, s32[12288]{0:T(1024)}, s32[1024]{0:T(1024)S(1)}, /*index=5*/f32[256,12]{...) while((s32[]{:T(128)}, f32[16,768,32]{1,0,2:T(8,128)S(1)}, ...), condition=%wide.region_1.4_spmd, body=%wide.region_0.3_spmd.sunk | while | flops 20943940 | bytes 5160803 | solution.py:130
  15.5 3.2 dynamic_update_slice.7
  26.3 3.2 dynamic_update_slice.7
  37.1 3.2 dynamic_update_slice.7
  47.8 3.2 dynamic_update_slice.7
  58.6 3.2 dynamic_update_slice.7
  69.3 3.2 dynamic_update_slice.7
  80.1 3.2 dynamic_update_slice.7
  90.9 3.2 dynamic_update_slice.7
  101.6 3.2 dynamic_update_slice.7
  112.4 3.2 dynamic_update_slice.7
  123.2 3.2 dynamic_update_slice.7
  133.9 3.2 dynamic_update_slice.7
  144.7 3.2 dynamic_update_slice.7
  155.5 3.2 dynamic_update_slice.7
  166.2 3.2 dynamic_update_slice.7
  177.0 3.2 dynamic_update_slice.7
  181.9 83.1 %all-reduce.1 = bf16[12288,32]{0,1:T(8,128)(2,1)S(1)} all-reduce(f32[12288,32]{0,1:T(8,128)S(1)} %bitcast.98), channel_id=1, replica_groups=mesh['ga'=8,'band'=4] {'ga'}, use_global_device_ids=true, to_apply=%region_2.0 | all-reduce | flops 393216 | bytes 2359296 | tf_op jit(solution)/shard_map/psum | solution.py:130
  265.0 16.8 %fusion.8 = bf16[1536,32]{0,1:T(8,128)(2,1)S(1)} fusion(bf16[1536,12288]{1,0:T(8,128)(2,1)} %all-gather.2.cloned.1.call-done, bf16[12288,32]{0,1:T(8,128)(2,1)S(1)} %all-reduce.1), kind=kOutput, calls=%fused_computation.49 | convolution fusion | flops 1208008704 | bytes 38633472 | tf_op jit(solution)/shard_map/dot_general | solution.py:133
  281.9 31.7 %all_gather.7 = bf16[12288,32]{0,1:T(8,128)(2,1)S(1)} all-gather(bf16[1536,32]{0,1:T(8,128)(2,1)S(1)} %fusion.8), channel_id=1, replica_groups=mesh['ga'=8,'band'=4] {'ga'}, dimensions={0}, use_global_device_ids=true | all-gather | bytes 884736 | tf_op jit(solution)/shard_map/all_gather | solution.py:134
  313.5 94.7 %while.28 = (s32[]{:T(128)}, f32[256,32]{0,1:T(8,128)S(1)}, s32[12288]{0:T(1024)}, s32[1024]{0:T(1024)S(1)}, f32[256,12]{0,1:T(8,128)S(1)}, /*index=5*/f32[3,256...) while((s32[]{:T(128)}, f32[256,32]{0,1:T(8,128)S(1)}, ...), condition=%wide.region_4.7_spmd, body=%wide.region_3.6_spmd.sunk | while | flops 20952132 | bytes 4767587 | solution.py:147
  321.2 1.6 gather_fusion.2
  344.9 1.6 gather_fusion.2
  350.8 1.6 gather_fusion.2
  (950 shorter events, 179.0 us)
Async XLA Ops:
  6.5 1.1 copy-start
  6.5 0.8 copy-start.5
  6.5 0.8 copy-start.4
  6.5 1.0 copy-start.3
  6.5 1.4 copy-start.1
  6.5 258.5 %all-gather.2.cloned.1.call-start = ((), (), s32[]{:S(2)}) async-start(), calls=%async_computation | async-start | bytes 47185920 | tf_op jit(solution)/shard_map/all_gather | solution.py:132
  180.2 0.8 copy-start.2
Sparse Core Ops, SparseCore 0:
  8.9 229.8 all-gather.1
where the time goes:
time: 418 us; the launch traced here: 416 us
  local copies, waits for them, and re-layouts  181 us (43%)
  blocking collectives  115 us (28%)
  other arithmetic  37.1 us (9%)
  loops' own time  35.3 us (8%)
  matrix products  33.3 us (8%)
  between operations  13.6 us (3%)
    psum x1, blocking collectives, shards(): summed = lax.psum(lax.map(one_block, starts).reshape(NPROJ, nbands), 'ga')  83.1 us
    dynamic_update_slice x32, local copies, waits for them, and re-layouts, shards(): summed = lax.psum(lax.map(one_block, starts).reshape(NPROJ, nbands), 'ga')  53.2 us
    gather x32, local copies, waits for them, and re-layouts, beta_atoms(): place = jnp.take(positions, atoms, axis=1)  35.9 us
    another operation x1, loops' own time, shards(): summed = lax.psum(lax.map(one_block, starts).reshape(NPROJ, nbands), 'ga')  32.7 us
    all_gather x1, blocking collectives, shards(): lax.all_gather(part, 'ga', axis=0, tiled=True)  31.7 us
    dynamic_slice x32, local copies, waits for them, and re-layouts, beta_atoms(): lax.dynamic_slice_in_dim(proj_atom, jnp.asarray(start).astype(jnp.int32),...  25 us
    gather x32, local copies, waits for them, and re-layouts, beta_atoms(): kind = jnp.take(species, atoms)  23.3 us
    dot_general x1, matrix products, shards(): jnp.dot(full_rows, proj_b, preferred_element_type=jnp.float32)  16.8 us
  transfers between devices with their start and end apart: 1, of which 0 were waited for; matrix products, arithmetic and copies ran while one was open for 34% of the time, Pallas kernels for 0%

commit v1 on v0

--- a/solution.py
+++ b/solution.py
@@ -127,7 +127,10 @@
             beta, coeffs, (((0,), (0,)), ((), ())), preferred_element_type=jnp.float32
         )
 
-    summed = lax.psum(lax.map(one_block, starts).reshape(NPROJ, nbands), "ga")
+    def make_zone_in(mat, peer_axis):
+        return lax.all_gather(mat, peer_axis).sum(axis=0)
+
+    summed = make_zone_in(lax.map(one_block, starts).reshape(NPROJ, nbands), "ga")
     proj_b = summed.astype(jnp.bfloat16)
     full_rows = lax.all_gather(coupling, "band", axis=1, tiled=True)
     mixed = jnp.dot(full_rows, proj_b, preferred_element_type=jnp.float32).astype(jnp.bfloat16)

time: 418 us -> 755 us (1.81)
  waiting for transfers between devices: 0.7 us -> 400 us
  blocking collectives: 115 us -> 32.3 us
  matrix products: 33.3 us -> 44.7 us
    all_gather x1, waiting for transfers between devices: 0.02 us -> 222 us  [shards(): full_rows = lax.all_gather(coupling, 'band', axis=1, tiled=True)]
    all_gather x0 -> x1, waiting for transfers between devices: none -> 178 us  [make_zone_in(): return lax.all_gather(mat, peer_axis).sum(axis=0)]
    psum x1 -> x0, blocking collectives: 83.1 us -> none  [shards(): summed = lax.psum(lax.map(one_block, starts).reshape(NPROJ, nbands), 'ga')]
    gather x32, local copies, waits for them, and re-layouts: 35.9 us -> 19.2 us  [beta_atoms(): place = jnp.take(positions, atoms, axis=1)]
    gather x32, local copies, waits for them, and re-layouts: 23.3 us -> 35.1 us  [beta_atoms(): kind = jnp.take(species, atoms)]
    dot_general x16, matrix products: 3.87 us -> 15.3 us  [one_block(): lax.dot_general(beta, coeffs, (((0,), (0,)), ((), ())), preferred_element...]
  transfers between devices with their start and end apart: 1 -> 2, of which waited for: 0 -> 2; matrix products, arithmetic and copies ran while one was open for 34% -> 1% of each run, Pallas kernels for 0% -> 0%
where the time goes in v1:
time: 755 us; the launch traced here: 750 us
  waiting for transfers between devices  400 us (53%)
  local copies, waits for them, and re-layouts  178 us (24%)
  matrix products  44.7 us (6%)
  other arithmetic  43.1 us (6%)
  loops' own time  38.5 us (5%)
  blocking collectives  32.3 us (4%)
  between operations  13.5 us (2%)
    all_gather x1, waiting for transfers between devices, shards(): full_rows = lax.all_gather(coupling, 'band', axis=1, tiled=True)  222 us
    all_gather x1, waiting for transfers between devices, make_zone_in(): return lax.all_gather(mat, peer_axis).sum(axis=0)  178 us
    dynamic_update_slice x32, local copies, waits for them, and re-layouts, shards(): lax.map(one_block, starts).reshape(NPROJ, nbands)  53.3 us
    another operation x1, loops' own time, shards(): lax.map(one_block, starts).reshape(NPROJ, nbands)  35.9 us
    gather x32, local copies, waits for them, and re-layouts, beta_atoms(): kind = jnp.take(species, atoms)  35.1 us
    all_gather x1, blocking collectives, shards(): lax.all_gather(part, 'ga', axis=0, tiled=True)  32.3 us
    dynamic_slice x32, local copies, waits for them, and re-layouts, beta_atoms(): lax.dynamic_slice_in_dim(proj_atom, jnp.asarray(start).astype(jnp.int32),...  25 us
    gather x32, local copies, waits for them, and re-layouts, beta_atoms(): place = jnp.take(positions, atoms, axis=1)  19.2 us
  transfers between devices with their start and end apart: 2, of which 2 were waited for; matrix products, arithmetic and copies ran while one was open for 1% of the time, Pallas kernels for 0%

profile of v1, /device:TPU:0, one launch (start us, length us, event | category | flops | bytes accessed | tf_op | source)
XLA Modules:
  0.0 750.3 jit_solution(11048882218585078548)
XLA Ops:
  8.5 199.7 %while.27 = (s32[]{:T(128)}, f32[16,768,32]{1,0,2:T(8,128)S(1)}, s32[16]{0:T(128)S(1)}, s32[12288]{0:T(1024)}, s32[1024]{0:T(1024)}, /*index=5*/f32[256,12]{0,1:...) while((s32[]{:T(128)}, f32[16,768,32]{1,0,2:T(8,128)S(1)}, ...), condition=%wide.region_1.4_spmd, body=%wide.region_0.3_spmd.sunk | while | flops 20943940 | bytes 5160803 | solution.py:133
  12.3 1.5 gather_fusion.1
  17.8 3.2 dynamic_update_slice.7
  30.3 3.2 dynamic_update_slice.7
  42.7 3.2 dynamic_update_slice.7
  55.2 3.2 dynamic_update_slice.7
  67.7 3.2 dynamic_update_slice.7
  80.2 3.2 dynamic_update_slice.7
  92.7 3.2 dynamic_update_slice.7
  105.1 3.2 dynamic_update_slice.7
  117.6 3.2 dynamic_update_slice.7
  130.1 3.2 dynamic_update_slice.7
  142.6 3.2 dynamic_update_slice.7
  155.1 3.2 dynamic_update_slice.7
  167.5 3.2 dynamic_update_slice.7
  180.0 3.2 dynamic_update_slice.7
  192.5 3.2 dynamic_update_slice.7
  205.0 3.2 dynamic_update_slice.7
  210.4 178.2 %all-gather.3.cloned.1.call-done = f32[8,12288,32]{1,2,0:T(8,128)} async-done(((f32[1,12288,32]{1,2,0:T(8,128)}), f32[8,12288,32]{1,2,0:T(8,128)}) %all-gather.3.cloned.1.call-update) | async-done | bytes 12582928 | tf_op jit(solution)/shard_map/all_gather | solution.py:131
  388.6 5.4 reduce_sum.9
  394.0 221.6 %all-gather.5.cloned.1.call-done = bf16[1536,12288]{1,0:T(8,128)(2,1)} async-done(((bf16[1536,3072]{1,0:T(8,128)(2,1)}), bf16[1536,12288]{1,0:T(8,128)(2,1)}) %all-gather.5.cloned.1.call-update) | async-done | bytes 37748752 | tf_op jit(solution)/shard_map/all_gather | solution.py:135
  615.6 16.8 %fusion.8 = bf16[1536,32]{0,1:T(8,128)(2,1)S(1)} fusion(bf16[1536,12288]{1,0:T(8,128)(2,1)} %all-gather.5.cloned.1.call-done, bf16[12288,32]{0,1:T(8,128)(2,1)S(1)} %reduce_sum.9), kind=kOutput, calls=%fused_computation.49 | convolution fusion | flops 1208008704 | bytes 38633472 | tf_op jit(solution)/shard_map/dot_general | solution.py:136
  632.4 32.3 %all_gather.11 = bf16[12288,32]{0,1:T(8,128)(2,1)S(1)} all-gather(bf16[1536,32]{0,1:T(8,128)(2,1)S(1)} %fusion.8), channel_id=1, replica_groups=mesh['ga'=8,'band'=4] {'ga'}, dimensions={0}, use_global_device_ids=true | all-gather | bytes 884736 | tf_op jit(solution)/shard_map/all_gather | solution.py:137
  664.7 78.1 %while.28 = (s32[]{:T(128)}, f32[256,32]{0,1:T(8,128)S(1)}, s32[12288]{0:T(1024)}, s32[1024]{0:T(1024)S(1)}, f32[256,12]{0,1:T(8,128)S(1)}, /*index=5*/f32[3,256...) while((s32[]{:T(128)}, f32[256,32]{0,1:T(8,128)S(1)}, ...), condition=%wide.region_4.7_spmd, body=%wide.region_3.6_spmd.sunk | while | flops 20952132 | bytes 4767587 | solution.py:150
  (949 shorter events, 191.2 us)
Async XLA Ops:
  6.5 1.7 copy-start
  6.5 382.1 %all-gather.3.cloned.1.call-start = ((), (), s32[]{:S(2)}) async-start(), calls=%async_computation | async-start | bytes 14155776 | tf_op jit(solution)/shard_map/all_gather | solution.py:131
  208.2 2.2 copy-start.3
  209.7 405.9 %all-gather.5.cloned.1.call-start = ((), (), s32[]{:S(2)}) async-start(), calls=%async_computation.1 | async-start | bytes 47185920 | tf_op jit(solution)/shard_map/all_gather | solution.py:135
  394.0 270.7 %copy-start.2 = (s32[1024]{0:T(1024)S(1)}, s32[1024]{0:T(1024)}, u32[]{:S(2)}) copy-start(s32[1024]{0:T(1024)} %get-tuple-element.692) | copy-start | bytes 12292
  664.7 78.7 %copy-start.1 = (f32[12,128]{1,0:T(8,128)S(1)}, f32[12,128]{1,0:T(8,128)}, u32[]{:S(2)}) copy-start(f32[12,128]{1,0:T(8,128)} %param.21) | copy-start | bytes 18436
Sparse Core Ops, SparseCore 0:
  209.8 178.8 all-gather.2
  390.2 225.3 all-gather.4
